TPU v7x, 32 devices: a whole 2x2x4 slice. The times are simulated.
32 devices in a mesh: chan: 4 (over y, x), slab: 8 (over z, core).
Axes of the slice: x: 2, y: 2, z: 4, core: 2. Of those that a mesh axis runs over, the one named last changes fastest.
Arguments:
- flux: float32 [4, 512, 128], P('chan', 'slab'), may hold values from -6 to 6
- offsets: int32 [512, 128], P('slab'), may hold values from 0 to 8191
- counts: int32 [512], P('slab'), may hold values from 96 to 128
- dest_owner: int32 [512, 1], P('slab'), may hold values from 0 to 7; in each aligned block of 64 rows (0 to 63, 64 to 127, ...) at most 16 rows name the same one
- dest_tile: int32 [512], P('slab'), may hold values from 0 to 255
- dirty: float32 [4, 4096, 4096], P('chan', 'slab'), may hold values from -60 to 60
- psf_real: float32 [4, 8192, 8192], P('chan', None, 'slab'), may hold values from -96 to 96
- psf_imag: float32 [4, 8192, 8192], P('chan', None, 'slab'), may hold values from -96 to 96
Outputs:
- residual: float32 [4, 4096, 4096], P('chan', 'slab')
- rms_values: float32 [4], replicated
- peak_values: float32 [4], replicated
Inputs may be any that keep to these rules, and one draw needn't show every extreme that they name: `dest_owner`: among the 64 blocks of one device (aligned blocks of rows) at most 16 name the same owner, a bound that some device reaches. `counts`: slots at or beyond a block's count hold no component.
All inputs are finite; a program needn't handle non-finite values.
Results may differ from a plain program's by a relative error of at most 0.00005.
Values sent between devices are 32-bit elements; how exact they have to be, the bound alone decides.
A program may use at most 384 MiB of HBM per device.

v0:
```python
import math

import jax
import jax.numpy as jnp
from jax import lax
from jax.experimental import pallas as pl
from jax.experimental.pallas import tpu as pltpu
from jax.sharding import PartitionSpec as P

TILE_R = 64
TILE_C = 128


PRECISE = lax.Precision.HIGH


def factor(length):
    levels = length.bit_length() - 1
    outer_len = 2 ** ((levels + 1) // 2)
    return (outer_len, length // outer_len)


def rotation(count_one, count_two, length, sign):
    row_ids = jnp.arange(count_one, dtype=jnp.int32)[:, None]
    col_ids = jnp.arange(count_two, dtype=jnp.int32)[None, :]
    turn_count = row_ids * col_ids % length
    angles = turn_count.astype(jnp.float32) * (2.0 * math.pi / length)
    return (jnp.cos(angles), sign * jnp.sin(angles))


def table(count_one, count_two, length, sign):
    cosine, sine = rotation(count_one, count_two, length, sign)
    first = jnp.stack([cosine, sine], axis=1)
    second = jnp.stack([-sine, cosine], axis=1)
    return jnp.stack([first, second], axis=0)


def contract(pattern, first_op, second_op):
    return jnp.einsum(pattern, first_op, second_op, precision=PRECISE)


def twiddle(values, phases):
    phase_re, phase_im = phases
    value_re = values[0]
    value_im = values[1]
    return jnp.stack(
        [value_re * phase_re - value_im * phase_im, value_re * phase_im + value_im * phase_re]
    )


def widen(phases):
    return (phases[0][:, :, None], phases[1][:, :, None])


def paint_kernel(starts, tile_cols, rows_ref, cols_ref, amounts_ref, image_ref):
    step = pl.program_id(0)
    image_ref[...] = jnp.zeros_like(image_ref)
    comp_slots = rows_ref.shape[-1]
    row_iota = lax.broadcasted_iota(jnp.int32, (TILE_R, comp_slots), 0)
    col_iota = lax.broadcasted_iota(jnp.int32, (TILE_C, comp_slots), 0)

    def add_block(index, carry):
        spread = jnp.where(row_iota == rows_ref[index], amounts_ref[index], 0.0)
        marks = (col_iota == cols_ref[index]).astype(jnp.float32)
        tile = lax.dot_general(
            spread,
            marks,
            (((1,), (1,)), ((), ())),
            precision=lax.Precision.HIGHEST,
            preferred_element_type=jnp.float32,
        )
        place = pl.ds(pl.multiple_of(tile_cols[index] * TILE_C, TILE_C), TILE_C)
        image_ref[:, place] = image_ref[:, place] + tile
        return carry

    lax.fori_loop(starts[step], starts[step + 1], add_block, 0)


def paint(pixels, amounts, width):
    blocks, comp_slots = pixels.shape
    bands = width // TILE_R
    band = pixels[:, 0] // (TILE_R * width)
    order = jnp.argsort(band)
    edges = jnp.arange(bands + 1, dtype=jnp.int32)
    starts = jnp.sum((band[None, :] < edges[:, None]).astype(jnp.int32), axis=1)
    pixels = pixels[order]
    amounts = amounts[order]
    tile_cols = pixels[:, 0] % width // TILE_C
    rows = (pixels // width % TILE_R).reshape(blocks, 1, comp_slots)
    cols = (pixels % TILE_C).reshape(blocks, 1, comp_slots)
    whole = pl.BlockSpec((blocks, 1, comp_slots), lambda step, *_: (0, 0, 0))
    return pl.pallas_call(
        paint_kernel,
        out_shape=jax.ShapeDtypeStruct((width, width), jnp.float32),
        grid_spec=pltpu.PrefetchScalarGridSpec(
            num_scalar_prefetch=2,
            grid=(bands,),
            in_specs=[whole, whole, whole],
            out_specs=pl.BlockSpec((TILE_R, width), lambda step, *_: (step, 0)),
        ),
    )(starts, tile_cols, rows, cols, amounts.reshape(blocks, 1, comp_slots))


def local_table(width, length, first_col, col_count):
    low_len = 2 ** ((width.bit_length() - 1) // 2)
    col_ids = first_col + jnp.arange(col_count, dtype=jnp.int32)[None, :]

    def phases(points):
        turns = points[:, None] * col_ids % length
        angles = turns.astype(jnp.float32) * (2.0 * math.pi / length)
        return jnp.cos(angles), -jnp.sin(angles)

    low_re, low_im = phases(jnp.arange(low_len, dtype=jnp.int32))
    high_re, high_im = phases(jnp.arange(width // low_len, dtype=jnp.int32) * low_len)
    low_re, low_im = low_re[None], low_im[None]
    high_re, high_im = high_re[:, None], high_im[:, None]
    real = (high_re * low_re - high_im * low_im).reshape(width, col_count)
    imag = (high_re * low_im + high_im * low_re).reshape(width, col_count)
    return real, imag


def local_columns(image, length, first_col, col_count):
    real, imag = local_table(image.shape[1], length, first_col, col_count)
    return jnp.stack([contract("rx,xc->rc", image, real), contract("rx,xc->rc", image, imag)])


def forward_cols(values, length):
    outer_len, inner_len = factor(length)
    col_count = values.shape[2]
    pieces = values.reshape(2, outer_len // 2, inner_len, col_count)
    partial_sum = contract(
        "sabc,satk->tkbc", pieces, table(outer_len // 2, outer_len, outer_len, -1.0)
    )
    partial_sum = twiddle(partial_sum, widen(rotation(outer_len, inner_len, length, -1.0)))
    result = contract("skbc,sbtj->tjkc", partial_sum, table(inner_len, inner_len, inner_len, -1.0))
    return result.reshape(2, length, col_count)


def inverse_cols(values, length):
    outer_len, inner_len = factor(length)
    col_count = values.shape[2]
    pieces = values.reshape(2, outer_len, inner_len, col_count)
    partial_sum = contract("sabc,sate->tebc", pieces, table(outer_len, outer_len, outer_len, 1.0))
    partial_sum = twiddle(partial_sum, widen(rotation(outer_len, inner_len, length, 1.0)))
    result = contract(
        "sebc,sbtd->tdec", partial_sum, table(inner_len, inner_len // 2, inner_len, 1.0)
    )
    return result.reshape(2, length // 2, col_count) * (1.0 / length)


def inverse_rows(values, length):
    outer_len, inner_len = factor(length)
    row_count = values.shape[1]
    pieces = values.reshape(2, row_count, outer_len, inner_len)
    partial_sum = contract("srab,sate->treb", pieces, table(outer_len, outer_len, outer_len, 1.0))
    partial_sum = twiddle(partial_sum, rotation(outer_len, inner_len, length, 1.0))
    real_table = table(inner_len, inner_len // 2, inner_len, 1.0)[:, :, 0]
    real_part = contract("sreb,sbd->rde", partial_sum, real_table)
    return real_part.reshape(row_count, length // 2) * (1.0 / length)


def on_device(flux, offsets, counts, dest_owner, dest_tile, dirty, psf_real, psf_imag):
    slab_count = lax.axis_size("slab")
    chan_local, rows_dev, row_width = dirty.shape
    length = 2 * row_width
    blocks, comp_slots = offsets.shape
    across = row_width // TILE_C
    tile_row = dest_tile // across
    tile_col = dest_tile % across
    pixels = (
        (dest_owner * rows_dev + tile_row[:, None] * TILE_R + offsets // TILE_C) * row_width
        + tile_col[:, None] * TILE_C
        + offsets % TILE_C
    )
    live_mask = jnp.arange(comp_slots, dtype=jnp.int32)[None, :] < counts[:, None]
    weights = jnp.where(live_mask, flux[0], 0.0)
    all_pixels = lax.all_gather(pixels, "slab", axis=0, tiled=True)
    all_weights = lax.all_gather(weights, "slab", axis=0, tiled=True)
    image = paint(all_pixels, all_weights, row_width)
    col_count = psf_real.shape[2]
    first_col = lax.axis_index("slab") * col_count
    columns = local_columns(image, length, first_col, col_count)
    spectrum = forward_cols(columns, length)
    filtered = twiddle(spectrum, (psf_real[0], psf_imag[0]))
    narrowed = inverse_cols(filtered, length)
    returned = lax.all_to_all(narrowed, "slab", split_axis=1, concat_axis=2, tiled=True)
    smeared = inverse_rows(returned, length)
    convolved = [dirty[0] - smeared]
    residual = jnp.stack(convolved)
    squares = jnp.sum(residual * residual, axis=(1, 2))
    peaks = jnp.max(jnp.abs(residual), axis=(1, 2))
    pixel_total = rows_dev * slab_count * row_width
    totals = lax.psum(squares, "slab")
    highest = lax.pmax(peaks, "slab")
    rms_values, peak_values = (
        lax.all_gather(jnp.sqrt(totals / pixel_total), "chan", axis=0, tiled=True),
        lax.all_gather(highest, "chan", axis=0, tiled=True),
    )
    return (residual, rms_values, peak_values)


def solution(mesh):
    placed = (
        P("chan", "slab", None),
        P("slab", None),
        P("slab"),
        P("slab", None),
        P("slab"),
        P("chan", "slab", None),
        P("chan", None, "slab"),
        P("chan", None, "slab"),
    )
    return jax.shard_map(
        on_device,
        mesh=mesh,
        in_specs=placed,
        out_specs=(P("chan", "slab", None), P(), P()),
        check_vma=False,
    )
```

profile of v0, /device:TPU:0, one launch (start us, length us, event | category | flops | bytes accessed | tf_op | source)
XLA Modules:
  0.0 2253.0 jit_solution(14210676139571772631)
XLA Ops:
  10.7 15.9 all_gather.12
  66.9 134.0 %shard_map.103 = f32[4096,4096]{1,0:T(8,128)} custom-call(s32[65]{0:T(128)} %convert_reduce_fusion.starts, s32[512]{0:T(512)} %add_select_fusion.9.tile_cols, s32[512,1,128]{2,1,0:T(1,128)} %get-tuple-element.23.rows_ref, s32[512,1,128]{2,1,0:T(1,128)} %get-tuple-element.22.cols_ref, f32[512,1,128]{2,1,0:T(1,128)} %bitcast.168), custom_call_target="tpu_custom_call" | custom-call | tf_op jit(solution)/shard_map/pallas_call | solution.py:92
  200.9 115.3 %convolution_bitcast_fusion.1 = f32[1,64,64,1024]{3,2,1,0:T(8,128)} fusion(f32[64,64,4096]{2,1,0:T(8,128)} %bitcast.28, f32[4096,1024,1]{1,0,2:T(8,128)} %bitcast.166), kind=kOutput, calls=%fused_computation.41 | convolution fusion | flops 103079215104 | bytes 100663296 | tf_op jit(solution)/shard_map/rx,xc->rc/dot_general | solution.py:39
  316.2 124.8 %convolution_bitcast_fusion = f32[1,64,64,1024]{3,2,1,0:T(8,128)} fusion(f32[64,64,4096]{2,1,0:T(8,128)} %bitcast.28, f32[4096,1024,1]{1,0,2:T(8,128)} %bitcast.165), kind=kOutput, calls=%fused_computation.40 | convolution fusion | flops 103079215104 | bytes 100663296 | tf_op jit(solution)/shard_map/rx,xc->rc/dot_general | solution.py:39
  441.0 23.6 %pad_maximum_fusion.2 = f32[2,64,64,1024]{3,2,1,0:T(8,128)} fusion(f32[1,64,64,1024]{3,2,1,0:T(8,128)} %convolution_bitcast_fusion, f32[1,64,64,1024]{3,2,1,0:T(8,128)} %convolution_bitcast_fusion.1), kind=kLoop, calls=%fused_computation.14 | loop fusion | flops 8388608 | bytes 67108864 | tf_op jit(solution)/shard_map/stack | solution.py:124
  464.7 57.4 %fusion.17 = f32[2,128,64,1024]{3,1,2,0:T(8,128)} fusion(f32[2,64,64,1024]{3,2,1,0:T(8,128)} %pad_maximum_fusion.2, f32[1,64,2,128]{3,1,0,2:T(8,128)S(1)} %get-tuple-element.29, f32[1,64,2,128]{3,1,0,2:T(8,128)S(1)} %get-tuple-element.28), kind=kOutput, calls=%fused_computation.33 | convolution fusion | flops 12884934656 | bytes 100794368 | tf_op jit(solution)/shard_map/sabc,satk->tkbc/dot_general | solution.py:39
  522.1 42.6 %multiply_subtract_fusion.1 = (f32[1,128,64,1024]{3,1,2,0:T(8,128)}, f32[1,128,64,1024]{3,1,2,0:T(8,128)}) fusion(f32[2,128,64,1024]{3,1,2,0:T(8,128)} %fusion.17, f32[128,64]{0,1:T(8,128)S(1)} %copy-done.24, f32[128,64]{0,1:T(8,128)S(1)} %copy-done.6), kind=kLoop, calls=%fused_computation.31 | loop fusion | flops 50331648 | bytes 134283264 | tf_op jit(solution)/shard_map/sub | solution.py:47
  564.7 45.1 %pad_maximum_fusion = f32[2,128,64,1024]{3,1,2,0:T(8,128)} fusion(f32[1,128,64,1024]{3,1,2,0:T(8,128)} %get-tuple-element.15, f32[1,128,64,1024]{3,1,2,0:T(8,128)} %get-tuple-element.14), kind=kLoop, calls=%fused_computation.2 | loop fusion | flops 16777216 | bytes 134217728 | tf_op jit(solution)/shard_map/stack | solution.py:46
  609.9 82.2 %fusion.20 = f32[2,64,128,1024]{3,1,2,0:T(8,128)} fusion(f32[2,128,64,1024]{3,1,2,0:T(8,128)} %pad_maximum_fusion, f32[1,64,2,64]{1,3,0,2:T(8,128)S(1)} %get-tuple-element.27, f32[1,64,2,64]{1,3,0,2:T(8,128)S(1)} %get-tuple-element.26), kind=kOutput, calls=%fused_computation.34 | convolution fusion | flops 12884918272 | bytes 134283264 | tf_op jit(solution)/shard_map/skbc,sbtj->tjkc/dot_general | solution.py:39
  692.1 43.5 %fusion.113 = (f32[1,64,128,1024]{3,1,2,0:T(8,128)}, f32[1,64,128,1024]{3,1,2,0:T(8,128)}) fusion(f32[2,64,128,1024]{3,1,2,0:T(8,128)} %fusion.20), kind=kLoop, calls=%fused_computation.215 | loop fusion | bytes 134217728 | tf_op jit(solution)/shard_map/slice | solution.py:44
  735.6 35.1 %copy.72 = f32[1,64,128,1024]{3,2,1,0:T(8,128)} copy(f32[1,64,128,1024]{3,1,2,0:T(8,128)} %get-tuple-element.16) | data formatting | bytes 67108864 | tf_op jit(solution)/shard_map/slice | solution.py:44
  770.8 36.1 %copy.73 = f32[1,64,128,1024]{3,2,1,0:T(8,128)} copy(f32[1,64,128,1024]{3,1,2,0:T(8,128)S(1)} %copy-done.1) | data formatting | bytes 67108864 | tf_op jit(solution)/shard_map/slice | solution.py:45
  806.9 64.5 %fusion.11 = (f32[1,8192,1024]{2,1,0:T(8,128)}, f32[1,8192,1024]{2,1,0:T(8,128)}) fusion(f32[1,8192,1024]{2,1,0:T(8,128)} %param.15, f32[1,64,128,1024]{3,2,1,0:T(8,128)} %copy.73, f32[1,8192,1024]{2,1,0:T(8,128)} %param.14, f32[1,64,128,1024]{3,2,1,0:T(8,128)} %copy.72), kind=kLoop, calls=%fused_computation.21 | loop fusion | flops 50331648 | bytes 201326592 | tf_op jit(solution)/shard_map/sub | solution.py:47
  871.4 35.2 %copy.74 = f32[1,128,64,1024]{3,1,0,2:T(8,128)} copy(f32[1,128,64,1024]{3,2,1,0:T(8,128)} %bitcast.164) | data formatting | bytes 67108864 | tf_op jit(solution)/shard_map/stack | solution.py:46
  906.6 36.1 %copy.75 = f32[1,128,64,1024]{3,1,0,2:T(8,128)} copy(f32[1,128,64,1024]{3,2,1,0:T(8,128)S(1)} %bitcast.163) | data formatting | bytes 67108864 | tf_op jit(solution)/shard_map/stack | solution.py:46
  942.8 56.2 %fusion.16 = f32[2,128,64,1024]{3,1,2,0:T(8,128)} fusion(f32[1,128,64,1024]{3,1,0,2:T(8,128)} %copy.75, f32[1,128,64,1024]{3,1,0,2:T(8,128)} %copy.74, f32[1,128,2,128]{1,3,0,2:T(8,128)S(1)} %get-tuple-element.25, f32[1,128,2,128]{1,3,0,2:T(8,128)S(1)} %get-tuple-element.24), kind=kOutput, calls=%fused_computation.32 | convolution fusion | flops 25786646528 | bytes 134479872 | tf_op jit(solution)/shard_map/sabc,sate->tebc/dot_general | solution.py:39
  999.0 42.4 %multiply_subtract_fusion = (f32[1,128,64,1024]{3,1,2,0:T(8,128)}, f32[1,128,64,1024]{3,1,2,0:T(8,128)}) fusion(f32[2,128,64,1024]{3,1,2,0:T(8,128)} %fusion.16, f32[128,64]{0,1:T(8,128)S(1)} %copy-done.13, f32[128,64]{0,1:T(8,128)S(1)} %copy-done.7), kind=kLoop, calls=%fused_computation.29 | loop fusion | flops 50331648 | bytes 134283264 | tf_op jit(solution)/shard_map/sub | solution.py:47
  1041.5 45.1 %pad_maximum_fusion.1 = f32[2,128,64,1024]{3,1,2,0:T(8,128)} fusion(f32[1,128,64,1024]{3,1,2,0:T(8,128)} %get-tuple-element.13, f32[1,128,64,1024]{3,1,2,0:T(8,128)} %get-tuple-element.12), kind=kLoop, calls=%fused_computation.7 | loop fusion | flops 16777216 | bytes 134217728 | tf_op jit(solution)/shard_map/stack | solution.py:46
  1086.7 73.9 %bitcast_multiply_fusion = f32[2,32,128,1024]{3,1,2,0:T(8,128)} fusion(f32[2,128,64,1024]{3,1,2,0:T(8,128)} %pad_maximum_fusion.1, f32[1,64,2,32]{1,3,0,2:T(8,128)S(1)} %get-tuple-element.31, f32[1,64,2,32]{1,3,0,2:T(8,128)S(1)} %get-tuple-element.30), kind=kOutput, calls=%fused_computation.18 | convolution fusion | flops 6450847744 | bytes 100696064 | tf_op jit(solution)/shard_map/sebc,sbtd->tdec/dot_general | solution.py:39
  1160.6 32.0 %copy.77 = f32[2,32,128,1024]{3,2,1,0:T(8,128)} copy(f32[2,32,128,1024]{3,1,2,0:T(8,128)} %bitcast_multiply_fusion) | data formatting | bytes 67108864 | tf_op jit(solution)/shard_map/mul | solution.py:148
  1192.5 55.0 %copy.78 = f32[2,4096,1024]{2,0,1:T(2,128)} copy(f32[2,4096,1024]{2,1,0:T(8,128)} %bitcast.160) | data formatting | bytes 67108864 | tf_op jit(solution)/shard_map/mul | solution.py:148
  1255.7 722.5 %all-to-all-done = f32[2,4096,1024]{2,0,1:T(2,128)} async-done(((f32[2,4096,1024]{2,0,1:T(2,128)}), f32[2,4096,1024]{2,0,1:T(2,128)}, u32[]{:S(2)}, u32[]{:S(2)}) %all-to-all-start) | async-done | bytes 33554464 | tf_op jit(solution)/shard_map/all_to_all | solution.py:186
  1978.2 30.5 %copy.79 = f32[2,4096,1024]{2,1,0:T(8,128)} copy(f32[2,4096,1024]{2,0,1:T(2,128)} %all-to-all-done) | data formatting | bytes 67108864 | tf_op jit(solution)/shard_map/all_to_all | solution.py:186
  2008.7 32.0 %copy.80 = f32[2,512,8,1024]{1,3,2,0:T(8,128)} copy(f32[2,512,8,1024]{3,1,2,0:T(8,128)} %bitcast.161) | data formatting | bytes 67108864 | tf_op jit(solution)/shard_map/all_to_all | solution.py:186
  2040.7 34.7 %copy.81 = f32[2,512,128,64]{2,1,0,3:T(8,128)} copy(f32[2,512,128,64]{1,3,2,0:T(8,128)} %bitcast.162) | data formatting | bytes 67108864 | tf_op jit(solution)/shard_map/reshape | solution.py:154
  2075.5 27.6 %fusion.25 = f32[2,512,128,64]{1,2,3,0:T(8,128)} fusion(f32[2,512,128,64]{2,1,0,3:T(8,128)} %copy.81, f32[1,128,2,128]{1,3,0,2:T(8,128)S(1)} %copy-done.5, f32[1,128,2,128]{1,3,0,2:T(8,128)S(1)} %copy-done.3), kind=kOutput, calls=%fused_computation.35 | convolution fusion | flops 12884967424 | bytes 67371008 | tf_op jit(solution)/shard_map/srab,sate->treb/dot_general | solution.py:39
  2103.1 17.7 multiply_subtract_fusion.2
  2120.8 18.7 pad_maximum_fusion.3
  2139.5 32.2 %copy.82 = f32[2,512,128,64]{2,3,0,1:T(8,128)} copy(f32[2,512,128,64]{1,2,3,0:T(8,128)} %pad_maximum_fusion.3) | data formatting | bytes 67108864 | tf_op jit(solution)/shard_map/stack | solution.py:46
  2171.7 19.0 fusion.28
  2209.9 15.1 pmax.7
  2225.1 14.2 psum.7
  (102 shorter events, 91.2 us)
Async XLA Ops:
  441.0 23.7 %copy-start.21 = (f32[64,1,128]{2,0,1:T(8,128)S(1)}, f32[64,1,128]{2,0,1:T(8,128)}, u32[]{:S(2)}) copy-start(f32[64,1,128]{2,0,1:T(8,128)} %get-tuple-element.36) | copy-start | bytes 98308
  441.0 23.7 %copy-start.22 = (f32[64,1,128]{2,0,1:T(8,128)S(1)}, f32[64,1,128]{2,0,1:T(8,128)}, u32[]{:S(2)}) copy-start(f32[64,1,128]{2,0,1:T(8,128)} %get-tuple-element.37) | copy-start | bytes 98308
  441.0 23.6 %copy-start.23 = (f32[64,1,128]{2,0,1:T(8,128)S(1)}, f32[64,1,128]{2,0,1:T(8,128)}, u32[]{:S(2)}) copy-start(f32[64,1,128]{2,0,1:T(8,128)} %fusion.96) | copy-start | bytes 98308
  464.6 57.4 %copy-start.6 = (f32[128,64]{0,1:T(8,128)S(1)}, f32[128,64]{0,1:T(8,128)}, u32[]{:S(2)}) copy-start(f32[128,64]{0,1:T(8,128)} %get-tuple-element.39) | copy-start | bytes 98308
  464.7 57.4 %copy-start.24 = (f32[128,64]{0,1:T(8,128)S(1)}, f32[128,64]{0,1:T(8,128)}, u32[]{:S(2)}) copy-start(f32[128,64]{0,1:T(8,128)} %get-tuple-element.38) | copy-start | bytes 98308
  564.7 45.1 %copy-start.18 = (f32[64,1,64]{0,2,1:T(8,128)S(1)}, f32[64,1,64]{0,2,1:T(8,128)}, u32[]{:S(2)}) copy-start(f32[64,1,64]{0,2,1:T(8,128)} %get-tuple-element.40) | copy-start | bytes 49156
  564.7 45.2 %copy-start.19 = (f32[64,1,64]{0,2,1:T(8,128)S(1)}, f32[64,1,64]{0,2,1:T(8,128)}, u32[]{:S(2)}) copy-start(f32[64,1,64]{0,2,1:T(8,128)} %get-tuple-element.41) | copy-start | bytes 49156
  564.7 45.2 %copy-start.20 = (f32[64,1,64]{0,2,1:T(8,128)S(1)}, f32[64,1,64]{0,2,1:T(8,128)}, u32[]{:S(2)}) copy-start(f32[64,1,64]{0,2,1:T(8,128)} %fusion.95) | copy-start | bytes 49156
  735.6 35.2 %copy-start.1 = (f32[1,64,128,1024]{3,1,2,0:T(8,128)S(1)}, f32[1,64,128,1024]{3,1,2,0:T(8,128)}, u32[]{:S(2)}) copy-start(f32[1,64,128,1024]{3,1,2,0:T(8,128)} %get-tuple-element.17) | copy-start | bytes 100663296
  871.4 35.2 %copy-start = (f32[1,8192,1024]{2,1,0:T(8,128)S(1)}, f32[1,8192,1024]{2,1,0:T(8,128)}, u32[]{:S(2)}) copy-start(f32[1,8192,1024]{2,1,0:T(8,128)} %get-tuple-element.11) | copy-start | bytes 100663296
  906.6 36.1 %copy-start.15 = (f32[128,1,128]{0,2,1:T(8,128)S(1)}, f32[128,1,128]{0,2,1:T(8,128)}, u32[]{:S(2)}) copy-start(f32[128,1,128]{0,2,1:T(8,128)} %get-tuple-element.42) | copy-start | bytes 196612
  906.6 36.1 %copy-start.16 = (f32[128,1,128]{0,2,1:T(8,128)S(1)}, f32[128,1,128]{0,2,1:T(8,128)}, u32[]{:S(2)}) copy-start(f32[128,1,128]{0,2,1:T(8,128)} %get-tuple-element.43) | copy-start | bytes 196612
  906.6 36.1 %copy-start.17 = (f32[128,1,128]{0,2,1:T(8,128)S(1)}, f32[128,1,128]{0,2,1:T(8,128)}, u32[]{:S(2)}) copy-start(f32[128,1,128]{0,2,1:T(8,128)} %fusion.84) | copy-start | bytes 196612
  942.7 56.3 %copy-start.2 = (f32[1,128,2,128]{1,3,0,2:T(8,128)}, f32[1,128,2,128]{1,3,0,2:T(8,128)S(1)}, u32[]{:S(2)}) copy-start(f32[1,128,2,128]{1,3,0,2:T(8,128)S(1)} %get-tuple-element.24) | copy-start | bytes 393220
  942.8 56.3 %copy-start.4 = (f32[1,128,2,128]{1,3,0,2:T(8,128)}, f32[1,128,2,128]{1,3,0,2:T(8,128)S(1)}, u32[]{:S(2)}) copy-start(f32[1,128,2,128]{1,3,0,2:T(8,128)S(1)} %get-tuple-element.25) | copy-start | bytes 393220
  942.8 56.3 %copy-start.7 = (f32[128,64]{0,1:T(8,128)S(1)}, f32[128,64]{0,1:T(8,128)}, u32[]{:S(2)}) copy-start(f32[128,64]{0,1:T(8,128)} %get-tuple-element.39) | copy-start | bytes 98308
  942.8 56.3 %copy-start.13 = (f32[128,64]{0,1:T(8,128)S(1)}, f32[128,64]{0,1:T(8,128)}, u32[]{:S(2)}) copy-start(f32[128,64]{0,1:T(8,128)} %fusion.88) | copy-start | bytes 98308
  1041.5 45.1 %copy-start.25 = (f32[64,1,32]{0,2,1:T(8,128)S(1)}, f32[64,1,32]{0,2,1:T(8,128)}, u32[]{:S(2)}) copy-start(f32[64,1,32]{0,2,1:T(8,128)} %get-tuple-element.44) | copy-start | bytes 24580
  1041.5 45.2 %copy-start.26 = (f32[64,1,32]{0,2,1:T(8,128)S(1)}, f32[64,1,32]{0,2,1:T(8,128)}, u32[]{:S(2)}) copy-start(f32[64,1,32]{0,2,1:T(8,128)} %get-tuple-element.45) | copy-start | bytes 24580
  1041.5 45.2 %copy-start.27 = (f32[64,1,32]{0,2,1:T(8,128)S(1)}, f32[64,1,32]{0,2,1:T(8,128)}, u32[]{:S(2)}) copy-start(f32[64,1,32]{0,2,1:T(8,128)} %fusion.99) | copy-start | bytes 24580
  1086.7 73.9 %copy-start.9 = (f32[1,64,2,32]{1,3,0,2:T(8,128)}, f32[1,64,2,32]{1,3,0,2:T(8,128)S(1)}, u32[]{:S(2)}) copy-start(f32[1,64,2,32]{1,3,0,2:T(8,128)S(1)} %get-tuple-element.30) | copy-start | bytes 49156
  1086.7 73.9 %copy-start.11 = (f32[1,64,2,32]{1,3,0,2:T(8,128)}, f32[1,64,2,32]{1,3,0,2:T(8,128)S(1)}, u32[]{:S(2)}) copy-start(f32[1,64,2,32]{1,3,0,2:T(8,128)S(1)} %get-tuple-element.31) | copy-start | bytes 49156
  1247.6 7.5 copy-start.28
  1247.6 730.6 %all-to-all-start = ((f32[2,4096,1024]{2,0,1:T(2,128)}), f32[2,4096,1024]{2,0,1:T(2,128)}, u32[]{:S(2)}, u32[]{:S(2)}) async-start(f32[2,4096,1024]{2,0,1:T(2,128)} %copy.78), calls=%async_computation | async-start | bytes 67108864 | tf_op jit(solution)/shard_map/all_to_all | solution.py:186
  2040.7 34.7 %copy-start.3 = (f32[1,128,2,128]{1,3,0,2:T(8,128)S(1)}, f32[1,128,2,128]{1,3,0,2:T(8,128)}, u32[]{:S(2)}) copy-start(f32[1,128,2,128]{1,3,0,2:T(8,128)} %copy-done.2) | copy-start | bytes 393220
  2040.7 34.7 %copy-start.5 = (f32[1,128,2,128]{1,3,0,2:T(8,128)S(1)}, f32[1,128,2,128]{1,3,0,2:T(8,128)}, u32[]{:S(2)}) copy-start(f32[1,128,2,128]{1,3,0,2:T(8,128)} %copy-done.4) | copy-start | bytes 393220
  2075.4 27.7 %copy-start.8 = (f32[128,64]{0,1:T(8,128)S(1)}, f32[128,64]{0,1:T(8,128)}, u32[]{:S(2)}) copy-start(f32[128,64]{0,1:T(8,128)} %get-tuple-element.39) | copy-start | bytes 98308
  2075.4 27.7 %copy-start.14 = (f32[128,64]{0,1:T(8,128)S(1)}, f32[128,64]{0,1:T(8,128)}, u32[]{:S(2)}) copy-start(f32[128,64]{0,1:T(8,128)} %fusion.88) | copy-start | bytes 98308
  2139.5 32.2 %copy-start.10 = (f32[1,64,2,32]{1,3,0,2:T(8,128)S(1)}, f32[1,64,2,32]{1,3,0,2:T(8,128)}, u32[]{:S(2)}) copy-start(f32[1,64,2,32]{1,3,0,2:T(8,128)} %copy-done.9) | copy-start | bytes 49156
  2139.5 32.2 %copy-start.12 = (f32[1,64,2,32]{1,3,0,2:T(8,128)S(1)}, f32[1,64,2,32]{1,3,0,2:T(8,128)}, u32[]{:S(2)}) copy-start(f32[1,64,2,32]{1,3,0,2:T(8,128)} %copy-done.11) | copy-start | bytes 49156
where the time goes:
time: 2260 us; the launch traced here: 2250 us
  waiting for transfers between devices  722 us (32%)
  matrix products  556 us (25%)
  local copies, waits for them, and re-layouts  417 us (18%)
  other arithmetic  344 us (15%)
  Pallas kernels  134 us (6%)
  blocking collectives  69.8 us (3%)
    all_to_all x1, waiting for transfers between devices, on_device(): lax.all_to_all(narrowed, 'slab', split_axis=1, concat_axis=2, tiled=True)  722 us
    dot_general x8, matrix products, contract(): return jnp.einsum(pattern, first_op, second_op, precision=PRECISE)  556 us
    sub x4, other arithmetic, twiddle(): value_re * phase_re - value_im * phase_im  167 us
    pallas_call x1, Pallas kernels, paint(): pl.pallas_call(paint_kernel, out_shape=jax.ShapeDtypeStruct((width, width...  134 us
    another operation x3, other arithmetic, twiddle(): jnp.stack([value_re * phase_re - value_im * phase_im, value_re * phase_im...  109 us
    another operation x3, local copies, waits for them, and re-layouts, twiddle(): jnp.stack([value_re * phase_re - value_im * phase_im, value_re * phase_im...  103 us
    mul x2, local copies, waits for them, and re-layouts, inverse_cols(): return result.reshape(2, length // 2, col_count) * (1.0 / length)  87 us
    slice x2, local copies, waits for them, and re-layouts, twiddle(): value_re = values[0]  78.7 us
  transfers between devices with their start and end apart: 1, of which 1 were waited for; matrix products, arithmetic and copies ran while one was open for 0% of the time, Pallas kernels for 0%

commit v1 on v0

v1 whole, which is shorter than its diff:
```python
import math

import jax
import jax.numpy as jnp
from jax import lax
from jax.experimental import pallas as pl
from jax.experimental.pallas import tpu as pltpu
from jax.sharding import PartitionSpec as P


TILE_R = 64
TILE_C = 128
LANES = 128
PAINT = 32
BATCH = 64
NEAR = 16
PITCH = 72
ODD = 65
F32 = jnp.float32
BF16 = jnp.bfloat16
VMEM_LIMIT = 64 * 1024 * 1024 - 128 * 1024


def unit(turns, length, sign):
    angles = (turns % length).astype(F32) * (2.0 * math.pi / length)
    return jnp.cos(angles), sign * jnp.sin(angles)


def product(one, two):
    return one[0] * two[0] - one[1] * two[1], one[0] * two[1] + one[1] * two[0]


def high_part(values):
    return lax.reduce_precision(values, 8, 7)


def left_parts(values):
    high = high_part(values)
    low = values - high
    return jnp.concatenate([high, high, low], axis=-1).astype(BF16)


def right_parts(values):
    high = values.astype(BF16)
    low = (values - high.astype(F32)).astype(BF16)
    return jnp.concatenate([high, low, high], axis=0)


def dot(first, second):
    return lax.dot_general(
        first, second, (((1,), (0,)), ((), ())), preferred_element_type=F32
    )


def combine(both, conj):
    count = both.shape[0] // 2
    width = both.shape[1] // 2
    cos_re, cos_im = both[:count, :width], both[:count, width:]
    sin_re, sin_im = both[count:, :width], both[count:, width:]
    if conj:
        return cos_re + sin_im, cos_im - sin_re
    return cos_re - sin_im, cos_im + sin_re


def params():
    return pltpu.CompilerParams(
        dimension_semantics=("arbitrary",), vmem_limit_bytes=VMEM_LIMIT
    )


def cost(flops, moved):
    return pl.CostEstimate(flops=int(flops), bytes_accessed=int(moved), transcendentals=0)


def tile_kernel(rows_ref, cols_ref, amounts_ref, tiles_ref):
    slots = rows_ref.shape[-1]
    row_iota = lax.broadcasted_iota(jnp.int32, (TILE_R, slots), 0)
    col_iota = lax.broadcasted_iota(jnp.int32, (TILE_C, slots), 0)
    for index in range(PAINT):
        amounts = amounts_ref[index]
        high = amounts.astype(BF16).astype(F32)
        low = amounts - high
        here = row_iota == rows_ref[index]
        spread = jnp.concatenate(
            [jnp.where(here, high, 0.0), jnp.where(here, low, 0.0)], axis=0
        ).astype(BF16)
        marks = jnp.where(col_iota == cols_ref[index], 1.0, 0.0).astype(BF16)
        both = lax.dot_general(
            spread, marks, (((1,), (1,)), ((), ())), preferred_element_type=F32
        )
        tile = both[:TILE_R] + both[TILE_R:]
        tile_high = tile.astype(BF16)
        tile_low = (tile - tile_high.astype(F32)).astype(BF16)
        place = pl.ds(index * TILE_R, TILE_R)
        tiles_ref[place, :TILE_C] = tile_high
        tiles_ref[place, TILE_C:] = tile_low


def make_tiles(rows, cols, amounts):
    blocks, _, slots = rows.shape
    part = pl.BlockSpec((PAINT, 1, slots), lambda step: (step, 0, 0))
    return pl.pallas_call(
        tile_kernel,
        out_shape=jax.ShapeDtypeStruct((blocks * TILE_R, 2 * TILE_C), BF16),
        grid=(blocks // PAINT,),
        in_specs=[part, part, part],
        out_specs=pl.BlockSpec((PAINT * TILE_R, 2 * TILE_C), lambda step: (step, 0)),
        compiler_params=params(),
        cost_estimate=cost(blocks * 4e7, blocks * 4e4),
    )(rows, cols, amounts)


def row_kernel(bands, tile_cols, tiles_ref, basis_ref, turn_ref, out_ref):
    blocks = bands.shape[0]
    out_ref[...] = jnp.zeros_like(out_ref)
    size = BATCH * TILE_R

    def step_of(step, carry):
        start = pl.multiple_of(step * size, size)
        tiles = tiles_ref[pl.ds(start, size), :]
        values = dot(jnp.concatenate([tiles, tiles[:, :TILE_C]], axis=1), basis_ref[...])
        for index in range(BATCH):
            block = step * BATCH + index
            turn = turn_ref[pl.ds(tile_cols[block], 1), :]
            turn_re, turn_im = turn[:, :LANES], turn[:, LANES:]
            part = values[index * TILE_R : (index + 1) * TILE_R]
            part_re, part_im = part[:, :LANES], part[:, LANES:]
            place = pl.ds(pl.multiple_of(bands[block] * PITCH, 8), TILE_R)
            out_ref[0, place, :] += part_re * turn_re - part_im * turn_im
            out_ref[1, place, :] += part_re * turn_im + part_im * turn_re
        return carry

    lax.fori_loop(0, blocks // BATCH, step_of, 0)


def row_transform(bands, tile_cols, tiles, basis, turns, width, first, count):
    blocks = bands.shape[0]
    across = turns.shape[0]
    height = width // TILE_R * PITCH
    return pl.pallas_call(
        row_kernel,
        out_shape=jax.ShapeDtypeStruct((2, height, count * LANES), F32),
        grid_spec=pltpu.PrefetchScalarGridSpec(
            num_scalar_prefetch=2,
            grid=(count,),
            in_specs=[
                pl.BlockSpec(
                    tiles.shape, lambda step, *_: (0, 0), pipeline_mode=pl.Buffered(1)
                ),
                pl.BlockSpec((3 * TILE_C, 2 * LANES), lambda step, *_: (0, step + first)),
                pl.BlockSpec((across, 2 * LANES), lambda step, *_: (0, step + first)),
            ],
            out_specs=pl.BlockSpec((2, height, LANES), lambda step, *_: (0, 0, step)),
        ),
        compiler_params=params(),
        cost_estimate=cost(blocks * count * 3e7, width * count * 1024),
    )(bands, tile_cols, tiles, basis, turns)


def paired(re, im):
    rows, cols = re.shape
    both = jnp.stack(
        [re.reshape(rows, cols // LANES, LANES), im.reshape(rows, cols // LANES, LANES)], axis=2
    )
    return both.reshape(rows, 2 * cols)


def row_tables(first_col, col_count, length, across):
    cols = first_col + jnp.arange(col_count, dtype=jnp.int32)[None, :]
    fine = paired(*unit(jnp.arange(TILE_C, dtype=jnp.int32)[:, None] * cols, length, -1.0))
    high = high_part(fine)
    basis = jnp.concatenate([high, high, fine - high], axis=0).astype(BF16)
    points = jnp.arange(across, dtype=jnp.int32)[:, None] * TILE_C
    return basis, paired(*unit(points * cols, length, -1.0))


def paint_kernel(starts, tile_cols, rows_ref, cols_ref, amounts_ref, image_ref):
    step = pl.program_id(0)
    image_ref[...] = jnp.zeros_like(image_ref)
    slots = rows_ref.shape[-1]
    row_iota = lax.broadcasted_iota(jnp.int32, (TILE_R, slots), 0)
    col_iota = lax.broadcasted_iota(jnp.int32, (TILE_C, slots), 0)

    def add_block(index, carry):
        spread = jnp.where(row_iota == rows_ref[index], amounts_ref[index], 0.0)
        marks = (col_iota == cols_ref[index]).astype(F32)
        tile = lax.dot_general(
            spread,
            marks,
            (((1,), (1,)), ((), ())),
            precision=lax.Precision.HIGHEST,
            preferred_element_type=F32,
        )
        place = pl.ds(pl.multiple_of(tile_cols[index] * TILE_C, TILE_C), TILE_C)
        image_ref[:, place] = image_ref[:, place] + tile
        return carry

    lax.fori_loop(starts[step], starts[step + 1], add_block, 0)


def dense_rows(bands, tile_cols, rows, cols, amounts, width, first_col, col_count, length):
    blocks, _, slots = rows.shape
    band_count = width // TILE_R
    order = jnp.argsort(bands)
    edges = jnp.arange(band_count + 1, dtype=jnp.int32)
    starts = jnp.sum((bands[None, :] < edges[:, None]).astype(jnp.int32), axis=1)
    whole = pl.BlockSpec((blocks, 1, slots), lambda step, *_: (0, 0, 0))
    image = pl.pallas_call(
        paint_kernel,
        out_shape=jax.ShapeDtypeStruct((width, width), F32),
        grid_spec=pltpu.PrefetchScalarGridSpec(
            num_scalar_prefetch=2,
            grid=(band_count,),
            in_specs=[whole, whole, whole],
            out_specs=pl.BlockSpec((TILE_R, width), lambda step, *_: (step, 0)),
        ),
    )(starts, tile_cols[order], rows[order], cols[order], amounts[order])
    ids = first_col + jnp.arange(col_count, dtype=jnp.int32)[None, :]
    low_len = 2 ** ((width.bit_length() - 1) // 2)
    low = unit(jnp.arange(low_len, dtype=jnp.int32)[:, None] * ids, length, -1.0)
    high = unit(
        jnp.arange(width // low_len, dtype=jnp.int32)[:, None] * low_len * ids, length, -1.0
    )
    table = product([part[:, None] for part in high], [part[None] for part in low])
    table = [part.reshape(width, col_count) for part in table]
    made = jnp.stack([jnp.dot(image, part, precision=lax.Precision.HIGH) for part in table])
    made = made.reshape(2, band_count, TILE_R, col_count)
    made = jnp.pad(made, ((0, 0), (0, 0), (0, PITCH - TILE_R), (0, 0)))
    return made.reshape(2, band_count * PITCH, col_count)


def both_parts(ref, rows):
    return right_parts(jnp.concatenate([ref[0, rows, :], ref[1, rows, :]], axis=1))


def column_kernel(plan, owners, pieces, first, spread_ref, psf_re, psf_im, outer_ref, inner_ref, back_ref, *rest):
    outs, (work, psf, arrived) = rest[: len(plan)], rest[len(plan) :]
    inner = TILE_R
    half = spread_ref.shape[1] // PITCH
    outer = 2 * half
    step_id = pl.program_id(0)
    steps = pl.num_programs(0)

    def copies(step):
        slot = step % 2
        cols = pl.ds(pl.multiple_of((first + step) * LANES, LANES), LANES)
        return [
            pltpu.make_async_copy(
                source.at[:, :, cols],
                psf.at[slot, part, :, pl.ds(0, outer), :],
                arrived.at[slot, part],
            )
            for part, source in enumerate((psf_re, psf_im))
        ]

    @pl.when(step_id == 0)
    def _():
        for copy in copies(step_id):
            copy.start()

    @pl.when(step_id + 1 < steps)
    def _():
        for copy in copies(step_id + 1):
            copy.start()

    def forward(step, carry):
        for index in range(NEAR):
            place = step * NEAR + index
            values = both_parts(spread_ref, pl.ds(place, half, stride=PITCH))
            rows = pl.ds(place, outer, stride=ODD)
            work[0, rows, :], work[1, rows, :] = combine(dot(outer_ref[place], values), False)
        return carry

    lax.fori_loop(0, inner // NEAR, forward, 0)
    for copy in copies(step_id):
        copy.wait()
    slot = step_id % 2

    def middle(step, carry):
        for index in range(NEAR):
            place = step * NEAR + index
            rows = pl.ds(place * ODD, inner)
            re, im = combine(dot(inner_ref[...], both_parts(work, rows)), False)
            psf_re = psf[slot, 0, :, place, :]
            psf_im = psf[slot, 1, :, place, :]
            values = jnp.concatenate(
                [re * psf_re - im * psf_im, re * psf_im + im * psf_re], axis=1
            )
            values = right_parts(values)
            work[0, rows, :], work[1, rows, :] = combine(dot(inner_ref[...], values), True)
        return carry

    lax.fori_loop(0, outer // NEAR, middle, 0)

    def backward(step, carry):
        for index in range(NEAR):
            place = step * NEAR + index
            values = both_parts(work, pl.ds(place, outer, stride=ODD))
            rows = pl.ds(place, half, stride=ODD)
            work[0, rows, :], work[1, rows, :] = combine(dot(back_ref[place], values), False)
        return carry

    lax.fori_loop(0, inner // NEAR, backward, 0)
    span = inner // pieces
    runs = half // (2 * owners)
    for out, held in zip(outs, plan):
        for owner in range(owners):
            for spot, (side, piece) in enumerate(held):
                for part in range(2):
                    for run in range(runs):
                        source = ((side * owners + owner) * runs + run) * ODD + piece * span
                        target = (((owner * len(held) + spot) * 2 + part) * runs + run) * span
                        out[target : target + span, :] = work[part, source : source + span, :]


def column_stage(spread, psf_re, psf_im, tables, plan, owners, pieces, first, count):
    height = spread.shape[1]
    width = height // PITCH * TILE_R
    outer = 2 * width // TILE_R
    outer_table, inner_table, back_table = tables
    sizes = [width // 2 // pieces * len(held) * 2 for held in plan]

    def fixed(table):
        zeros = (0,) * table.ndim
        return pl.BlockSpec(table.shape, lambda step: zeros, pipeline_mode=pl.Buffered(1))

    def body(*refs):
        column_kernel(plan, owners, pieces, first, *refs)

    def by_turn(psf):
        return psf.reshape(TILE_R, outer, psf.shape[2])

    return pl.pallas_call(
        body,
        out_shape=[jax.ShapeDtypeStruct((size, count * LANES), F32) for size in sizes],
        grid=(count,),
        in_specs=[
            pl.BlockSpec((2, height, LANES), lambda step: (0, 0, step)),
            pl.BlockSpec(memory_space=pl.ANY),
            pl.BlockSpec(memory_space=pl.ANY),
            fixed(outer_table),
            fixed(inner_table),
            fixed(back_table),
        ],
        out_specs=[pl.BlockSpec((size, LANES), lambda step: (0, step)) for size in sizes],
        scratch_shapes=[
            pltpu.VMEM((2, outer * ODD, LANES), F32),
            pltpu.VMEM((2, 2, TILE_R, outer + 8, LANES), F32),
            pltpu.SemaphoreType.DMA((2, 2)),
        ],
        compiler_params=params(),
        cost_estimate=cost(count * 2.5e10, count * 2e7),
    )(spread, by_turn(psf_re), by_turn(psf_im), outer_table, inner_table, back_table)


def column_tables(width, length, half_id):
    inner = TILE_R
    half = width // inner
    outer = 2 * half
    fast = jnp.arange(inner, dtype=jnp.int32)
    slow = jnp.arange(half, dtype=jnp.int32)
    freq = jnp.arange(outer, dtype=jnp.int32)
    coarse = unit(freq[:, None] * slow[None, :], outer, -1.0)
    fine = unit(fast[:, None] * freq[None, :], length, -1.0)
    cosine, sine = product([part[None] for part in coarse], [part[:, :, None] for part in fine])
    outer_table = left_parts(jnp.concatenate([cosine, sine], axis=1))
    cosine, sine = unit(fast[:, None] * fast[None, :], inner, -1.0)
    inner_table = left_parts(jnp.concatenate([cosine, sine], axis=0))
    count = inner // 2
    last_table = left_parts(jnp.concatenate([cosine[:count], sine[:count]], axis=0))
    ranks = (slow + half // 2 * (1 - half_id)) % half
    coarse = unit(ranks[:, None] * freq[None, :], outer, 1.0)
    fine = unit(fast[:, None] * freq[None, :], length, 1.0)
    cosine, sine = product([part[None] for part in coarse], [part[:, None, :] for part in fine])
    back_table = left_parts(jnp.concatenate([cosine, sine], axis=1))
    return (outer_table, inner_table, back_table), last_table


def last_kernel(groups, signs, outer_ref, last_ref, *rest):
    ins, rest = rest[:groups], rest[groups:]
    base, (out_ref, flat, work, image) = rest[:-4], rest[-4:]
    owners, _, _, rows, lanes = ins[0].shape
    inner = TILE_R
    chunks = lanes // LANES
    turns = LANES // inner
    if rows < LANES:
        flat[...] = jnp.zeros_like(flat)
    for owner in range(owners):
        for group in range(groups):
            for chunk in range(chunks):
                start = ((owner * groups + group) * chunks + chunk) * turns
                lane = chunk * LANES
                for part in range(2):
                    values = ins[group][owner, 0, part, :, lane : lane + LANES].T
                    for turn in range(turns):
                        place = (start + turn) * PITCH
                        flat[part, place : place + inner, :rows] = values[
                            turn * inner : (turn + 1) * inner
                        ]
    half = flat.shape[1] // PITCH
    outer = 2 * half

    def forward(step, carry):
        for index in range(8):
            place = step * 8 + index
            values = both_parts(flat, pl.ds(place, half, stride=PITCH))
            span = pl.ds(place, outer, stride=ODD)
            work[0, span, :], work[1, span, :] = combine(dot(outer_ref[place], values), True)
        return carry

    lax.fori_loop(0, inner // 8, forward, 0)
    count = last_ref.shape[0] // 2

    def final(step, carry):
        for index in range(8):
            place = step * 8 + index
            both = dot(last_ref[...], both_parts(work, pl.ds(place * ODD, inner)))
            re, _ = combine(both, True)
            image[pl.ds(place, count, stride=outer + 8), :] = re * signs[index % 2]
        return carry

    lax.fori_loop(0, outer // 8, final, 0)
    runs, _, span, width = out_ref.shape
    for tile in range(width // LANES):
        place = tile * LANES // outer * (outer + 8) + tile * LANES % outer
        values = image[place : place + LANES, :].T
        cols = slice(tile * LANES, (tile + 1) * LANES)
        for run in range(runs):
            part = values[run * span : (run + 1) * span]
            if base:
                part = base[0][run, 0, :, cols] - part
            out_ref[run, 0, :, cols] = part


def last_stage(parts, spots, steps, span, outer_table, last_table, signs, base=()):
    owners, _, _, rows, lanes = parts[0].shape
    groups = len(parts)
    step_rows = min(rows, LANES)
    per = rows // step_rows
    width = owners * groups * lanes
    runs = step_rows // span

    def fixed(table):
        zeros = (0,) * table.ndim
        return pl.BlockSpec(table.shape, lambda step, *_: zeros, pipeline_mode=pl.Buffered(1))

    def part_spec(spot):
        return pl.BlockSpec(
            (owners, 1, 2, step_rows, lanes),
            lambda step, *_: (0, spot + step // per, 0, step % per, 0),
        )

    natural = pl.BlockSpec((runs, 1, span, width), lambda step, *_: (step % per, step // per, 0, 0))

    def body(*refs):
        last_kernel(groups, *refs)

    outer = 2 * width // TILE_R
    return pl.pallas_call(
        body,
        out_shape=jax.ShapeDtypeStruct((rows // span, steps, span, width), F32),
        grid_spec=pltpu.PrefetchScalarGridSpec(
            num_scalar_prefetch=1,
            grid=(steps * per,),
            in_specs=[fixed(outer_table), fixed(last_table)]
            + [part_spec(spot) for spot in spots]
            + [natural] * len(base),
            out_specs=natural,
            scratch_shapes=[
                pltpu.VMEM((2, width // TILE_R * PITCH, LANES), F32),
                pltpu.VMEM((2, outer * ODD, LANES), F32),
                pltpu.VMEM((width // outer * (outer + 8), LANES), F32),
            ],
        ),
        compiler_params=params(),
        cost_estimate=cost(steps * rows * 8e7, steps * rows * 5e4),
    )(signs, outer_table, last_table, *parts, *base)


def finish_kernel(*refs):
    base_ref, others, (out_ref, sum_ref, top_ref) = refs[0], refs[1:-3], refs[-3:]

    @pl.when(pl.program_id(0) == 0)
    def _():
        sum_ref[...] = jnp.zeros_like(sum_ref)
        top_ref[...] = jnp.zeros_like(top_ref)

    total = sum_ref[...]
    top = top_ref[...]
    span, width = base_ref.shape[2:]
    for number, other in enumerate(others):
        values = base_ref[0, number] - other[0, 0]
        out_ref[0, number] = values
        sizes = (span // 8, 8, width)
        total = total + jnp.sum((values * values).reshape(sizes), axis=0)
        top = jnp.maximum(top, jnp.max(jnp.abs(values).reshape(sizes), axis=0))
    sum_ref[...] = total
    top_ref[...] = top


def finish(base, others):
    runs, pieces, span, width = base.shape
    whole = pl.BlockSpec((1, pieces, span, width), lambda step: (step, 0, 0, 0))
    one = pl.BlockSpec((1, 1, span, width), lambda step: (step, 0, 0, 0))
    small = pl.BlockSpec((8, width), lambda step: (0, 0))
    return pl.pallas_call(
        finish_kernel,
        out_shape=[
            jax.ShapeDtypeStruct(base.shape, F32),
            jax.ShapeDtypeStruct((8, width), F32),
            jax.ShapeDtypeStruct((8, width), F32),
        ],
        grid=(runs,),
        in_specs=[whole] + [one] * pieces,
        out_specs=[whole, small, small],
        compiler_params=params(),
        cost_estimate=cost(base.size * 4, base.size * 12),
    )(base, *others)


def on_device(flux, offsets, counts, dest_owner, dest_tile, dirty, psf_real, psf_imag):
    slab_count = lax.axis_size("slab")
    slab_id = lax.axis_index("slab")
    _, rows_dev, width = dirty.shape
    length = 2 * width
    blocks_dev, slots = offsets.shape
    blocks = blocks_dev * slab_count
    across = width // TILE_C
    col_count = psf_real.shape[2]
    chunks = col_count // LANES
    first_col = slab_id * col_count
    owners = slab_count // 2
    half_id = slab_id // owners
    halves = [list(range(owners)), list(range(owners, slab_count))]
    partners = [(i, (i + owners) % slab_count) for i in range(slab_count)]

    live_mask = jnp.arange(slots, dtype=jnp.int32)[None, :] < counts[:, None]
    weights = jnp.where(live_mask, flux[0], 0.0)
    tile_count = (rows_dev // TILE_R) * across
    places = dest_owner * tile_count + dest_tile[:, None]
    packed = jnp.stack(
        [weights, offsets.astype(F32), jnp.broadcast_to(places, offsets.shape).astype(F32)], axis=1
    )
    packed = lax.all_gather(packed, "slab", axis=0, tiled=True)
    amounts = packed[:, 0:1]
    points = packed[:, 1:2].astype(jnp.int32)
    places = packed[:, 2, 0].astype(jnp.int32)
    rows, cols = points // TILE_C, points % TILE_C
    bands, tile_cols = places // across, places % across

    pieces = max(1, min(2, rows_dev // LANES))
    part_rows = rows_dev // pieces
    tables, last_table = column_tables(width, length, half_id)
    groups = 4 if chunks % 4 == 0 else 1
    sparse = blocks * TILE_R <= 8 * width
    if sparse:
        tiles = make_tiles(rows, cols, amounts)
        basis, turns = row_tables(first_col, col_count, length, across)
    count = chunks // groups
    every = tuple(range(pieces))

    def swap(part):
        return lax.all_to_all(part, "slab", 0, 0, axis_index_groups=halves, tiled=True)

    far, near = [], []
    for group in range(groups):
        first = group * count
        if sparse:
            spread = row_transform(bands, tile_cols, tiles, basis, turns, width, first, count)
        else:
            spread = dense_rows(
                bands, tile_cols, rows, cols, amounts, width, first_col, col_count, length
            )
        last = group == groups - 1
        sides = [[(side, piece) for piece in every] for side in range(2)]
        if last:
            plan = [[held] for held in sides[0]] + [sides[1]]
        elif group == 0:
            plan = [sides[0] + sides[1]]
        else:
            plan = sides
        made = column_stage(spread, psf_real, psf_imag, tables, plan, owners, pieces, first, count)
        made = [
            part.reshape(owners, len(held), 2, part_rows, count * LANES)
            for part, held in zip(made, plan)
        ]
        bands, *made = lax.optimization_barrier((bands, *made))
        if len(plan) > 1:
            near.append(made.pop())
        far.append([swap(part) for part in made])
    scale = 1.0 / (length * length)
    odd = jnp.where(half_id == 0, scale, -scale)
    signs = jnp.stack([jnp.full_like(odd, scale), odd])
    span = TILE_R // pieces
    final = (tables[0], last_table, signs)
    others = []
    for piece in every:
        parts = [held[0] for held in far[:-1]] + [far[-1][piece]]
        spots = [piece] * (groups - 1) + [0]
        made = last_stage(parts, spots, 1, span, *final)
        others.append(lax.ppermute(made, "slab", partners))
    near = [swap(part) for part in near]
    near = [held[0] for held in far[: groups - len(near)]] + near
    base = dirty.reshape(rows_dev // TILE_R, pieces, span, width)
    spots = [pieces] + [0] * (groups - 1) if groups > 1 else [0]
    base = last_stage(near, spots, pieces, span, *final, (base,))
    residual, sums, tops = finish(base, others)
    residual = residual.reshape(1, rows_dev, width)
    stats = jnp.stack([jnp.sum(sums), jnp.max(tops)])
    stats = lax.all_gather(stats, "slab", axis=0, tiled=False)
    total = rows_dev * slab_count * width
    stats = jnp.stack([jnp.sqrt(jnp.sum(stats[:, 0]) / total), jnp.max(stats[:, 1])])
    stats = lax.all_gather(stats, "chan", axis=0, tiled=False)
    rms_values, peak_values = stats[:, 0], stats[:, 1]
    return (residual, rms_values, peak_values)


def solution(mesh):
    placed = (
        P("chan", "slab", None),
        P("slab", None),
        P("slab"),
        P("slab", None),
        P("slab"),
        P("chan", "slab", None),
        P("chan", None, "slab"),
        P("chan", None, "slab"),
    )
    return jax.shard_map(
        on_device,
        mesh=mesh,
        in_specs=placed,
        out_specs=(P("chan", "slab", None), P(), P()),
        check_vma=False,
    )
```

time: 2260 us -> 1180 us (0.52)
  matrix products: 556 us -> 0 us
  waiting for transfers between devices: 722 us -> 287 us
  local copies, waits for them, and re-layouts: 417 us -> 5.43 us
  blocking collectives: 69.8 us -> 407 us
  other arithmetic: 344 us -> 35.5 us
  Pallas kernels: 134 us -> 422 us
    all_to_all x1, waiting for transfers between devices: 722 us -> 8.11 us  [swap(): lax.all_to_all(part, 'slab', 0, 0, axis_index_groups=halves, tiled=True)]
    dot_general x8 -> x0, matrix products: 556 us -> none  [contract(): return jnp.einsum(pattern, first_op, second_op, precision=PRECISE)]
    all_to_all x0 -> x7, blocking collectives: none -> 364 us  [swap(): lax.all_to_all(part, 'slab', 0, 0, axis_index_groups=halves, tiled=True)]
    pallas_call x1 -> x13, Pallas kernels: 134 us -> 422 us  [the longest x4 178 us: column_stage(): pl.pallas_call(body, out_shape=[jax.ShapeDtypeStruct((size, count * LANES...]
    ppermute x0 -> x2, waiting for transfers between devices: none -> 279 us  [on_device(): others.append(lax.ppermute(made, 'slab', partners))]
    sub x5 -> x2, other arithmetic: 179 us -> 3.4 us  [product(): one[0] * two[0] - one[1] * two[1]]
    another operation x8 -> x10, other arithmetic: 133 us -> 5.26 us  [the longest x3 109 us: twiddle(): jnp.stack([value_re * phase_re - value_im * phase_im, value_re * phase_im...]
    slice x5 -> x4, local copies, waits for them, and re-layouts: 115 us -> 1.44 us  [the longest x1 0.73 us: on_device(): amounts = packed[:, 0:1]]
  transfers between devices with their start and end apart: 1 -> 3, of which waited for: 1 -> 3; matrix products, arithmetic and copies ran while one was open for 0% -> 0% of each run, Pallas kernels for 0% -> 8%
where the time goes in v1:
time: 1180 us; the launch traced here: 1170 us
  Pallas kernels  422 us (36%)
  blocking collectives  407 us (34%)
  waiting for transfers between devices  287 us (24%)
  other arithmetic  35.5 us (3%)
    all_to_all x7, blocking collectives, swap(): lax.all_to_all(part, 'slab', 0, 0, axis_index_groups=halves, tiled=True)  364 us
    ppermute x2, waiting for transfers between devices, on_device(): others.append(lax.ppermute(made, 'slab', partners))  279 us
    pallas_call x4, Pallas kernels, column_stage(): pl.pallas_call(body, out_shape=[jax.ShapeDtypeStruct((size, count * LANES...  178 us
    pallas_call x4, Pallas kernels, row_transform(): pl.pallas_call(row_kernel, out_shape=jax.ShapeDtypeStruct((2, height, cou...  120 us
    pallas_call x3, Pallas kernels, last_stage(): pl.pallas_call(body, out_shape=jax.ShapeDtypeStruct((rows // span, steps,...  97.4 us
    unnamed x2, blocking collectives  25.7 us
  transfers between devices with their start and end apart: 3, of which 3 were waited for; matrix products, arithmetic and copies ran while one was open for 0% of the time, Pallas kernels for 8%

profile of v1, /device:TPU:0, one launch (start us, length us, event | category | flops | bytes accessed | tf_op | source)
XLA Modules:
  0.0 1167.7 jit_solution(3647243664958476942)
XLA Ops:
  3.6 17.2 %all_gather.15 = f32[512,3,128]{2,0,1:T(8,128)S(1)} all-gather(f32[64,3,128]{2,0,1:T(8,128)S(1)} %pad_maximum_fusion.7), channel_id=1, replica_groups=mesh['chan'=4,'slab'=8] {'slab'}, dimensions={0}, use_global_device_ids=true | all-gather | bytes 884736 | tf_op jit(solution)/shard_map/all_gather | solution.py:544
  31.4 2.8 multiply_subtract_fusion
  34.2 2.4 reduce-precision_convert_fusion
  36.7 5.7 pad_maximum_fusion.1.refs_3_.refs_1_
  46.3 3.1 pad_maximum_fusion.2.refs_5_
  49.4 16.5 %shard_map.103.tiles_ref = bf16[32768,256]{1,0:T(8,128)(2,1)} custom-call(s32[512,1,128]{2,1,0:T(1,128)} %and_select_fusion.1.rows_ref, s32[512,1,128]{2,1,0:T(1,128)} %get-tuple-element.49.cols_ref, f32[512,1,128]{2,1,0:T(1,128)} %bitcast.45), custom_call_target="tpu_custom_call" | custom-call | flops 20480000000 | bytes 20480000 | tf_op jit(solution)/shard_map/pallas_call | solution.py:102
  65.9 29.8 %shard_map.104.refs_0_ = f32[2,4608,256]{2,1,0:T(8,128)} custom-call(s32[512]{0:T(512)} %get-tuple-element.33.bands, s32[512]{0:T(512)} %get-tuple-element.71.tile_cols, bf16[32768,256]{1,0:T(8,128)(2,1)} %shard_map.103.tiles_ref, bf16[384,2048]{1,0:T(8,128)(2,1)} %pad_maximum_fusion.4.basis_ref, f32[32,2048]{1,0:T(8,128)} %reshape.427.turn_ref), custom_call_target="tpu_custom_call" | custom-call | flops 30720000000 | bytes 8388608 | tf_op jit(solution)/shard_map/pallas_call | solution.py:140
  95.7 44.4 %shard_map.105 = f32[8192,256]{1,0:T(8,128)} custom-call(f32[2,4608,256]{2,1,0:T(8,128)} %shard_map.104.refs_0_, f32[64,128,1024]{2,1,0:T(8,128)} %bitcast.46, f32[64,128,1024]{2,1,0:T(8,128)} %bitcast.50, bf16[64,256,192]{2,1,0:T(8,128)(2,1)} %pad_maximum_fusion.1.refs_3_.refs_1_, bf16[128,192]{1,0:T(8,128)(2,1)} %pad_maximum_fusion.9.refs_4_, ...), custom_call_target="tpu_custom_call" | custom-call | flops 49999998976 | bytes 40000000 | tf_op jit(solution)/shard_map/pallas_call | solution.py:333
  140.1 29.9 %shard_map.106.refs_0_ = f32[2,4608,256]{2,1,0:T(8,128)} custom-call(s32[512]{0:T(512)} %get-tuple-element.33.bands, s32[512]{0:T(512)} %get-tuple-element.71.tile_cols, bf16[32768,256]{1,0:T(8,128)(2,1)} %shard_map.103.tiles_ref, bf16[384,2048]{1,0:T(8,128)(2,1)} %pad_maximum_fusion.4.basis_ref, f32[32,2048]{1,0:T(8,128)} %reshape.427.turn_ref), custom_call_target="tpu_custom_call" | custom-call | flops 30720000000 | bytes 8388608 | tf_op jit(solution)/shard_map/pallas_call | solution.py:140
  170.0 44.5 %shard_map.107 = (f32[4096,256]{1,0:T(8,128)}, f32[4096,256]{1,0:T(8,128)}) custom-call(f32[2,4608,256]{2,1,0:T(8,128)} %shard_map.106.refs_0_, f32[64,128,1024]{2,1,0:T(8,128)} %bitcast.47, f32[64,128,1024]{2,1,0:T(8,128)} %bitcast.51, bf16[64,256,192]{2,1,0:T(8,128)(2,1)} %pad_maximum_fusion.1.refs_3_.refs_1_, bf16[128,192]{1,0:T(8,128)(2,1)} %pad_maximum_fusion.9.refs_4_, ...), custom_call_target="tpu_custom_call" | custom-call | flops 49999998976 | bytes 40000000 | tf_op jit(solution)/shard_map/pallas_call | solution.py:333
  214.6 29.9 %shard_map.108.refs_0_ = f32[2,4608,256]{2,1,0:T(8,128)} custom-call(s32[512]{0:T(512)} %get-tuple-element.33.bands, s32[512]{0:T(512)} %get-tuple-element.71.tile_cols, bf16[32768,256]{1,0:T(8,128)(2,1)} %shard_map.103.tiles_ref, bf16[384,2048]{1,0:T(8,128)(2,1)} %pad_maximum_fusion.4.basis_ref, f32[32,2048]{1,0:T(8,128)} %reshape.427.turn_ref), custom_call_target="tpu_custom_call" | custom-call | flops 30720000000 | bytes 8388608 | tf_op jit(solution)/shard_map/pallas_call | solution.py:140
  244.5 44.3 %shard_map.109 = (f32[4096,256]{1,0:T(8,128)}, f32[4096,256]{1,0:T(8,128)}) custom-call(f32[2,4608,256]{2,1,0:T(8,128)} %shard_map.108.refs_0_, f32[64,128,1024]{2,1,0:T(8,128)} %bitcast.48, f32[64,128,1024]{2,1,0:T(8,128)} %bitcast.52, bf16[64,256,192]{2,1,0:T(8,128)(2,1)} %pad_maximum_fusion.1.refs_3_.refs_1_, bf16[128,192]{1,0:T(8,128)(2,1)} %pad_maximum_fusion.9.refs_4_, ...), custom_call_target="tpu_custom_call" | custom-call | flops 49999998976 | bytes 40000000 | tf_op jit(solution)/shard_map/pallas_call | solution.py:333
  288.8 29.9 %shard_map.110.refs_0_ = f32[2,4608,256]{2,1,0:T(8,128)} custom-call(s32[512]{0:T(512)} %get-tuple-element.33.bands, s32[512]{0:T(512)} %get-tuple-element.71.tile_cols, bf16[32768,256]{1,0:T(8,128)(2,1)} %shard_map.103.tiles_ref, bf16[384,2048]{1,0:T(8,128)(2,1)} %pad_maximum_fusion.4.basis_ref, f32[32,2048]{1,0:T(8,128)} %reshape.427.turn_ref), custom_call_target="tpu_custom_call" | custom-call | flops 30720000000 | bytes 8388608 | tf_op jit(solution)/shard_map/pallas_call | solution.py:140
  318.8 44.3 %shard_map.111 = (f32[2048,256]{1,0:T(8,128)}, f32[2048,256]{1,0:T(8,128)}, f32[4096,256]{1,0:T(8,128)}) custom-call(f32[2,4608,256]{2,1,0:T(8,128)} %shard_map.110.refs_0_, f32[64,128,1024]{2,1,0:T(8,128)} %bitcast.49, f32[64,128,1024]{2,1,0:T(8,128)} %bitcast.53, bf16[64,256,192]{2,1,0:T(8,128)(2,1)} %pad_maximum_fusion.1.refs_3_.refs_1_, ...), custom_call_target="tpu_custom_call" | custom-call | flops 49999998976 | bytes 40000000 | tf_op jit(solution)/shard_map/pallas_call | solution.py:333
  363.1 30.5 %all_to_all.40.refs_6_ = f32[4,1,2,256,256]{4,3,2,1,0:T(8,128)} all-to-all(f32[4,1,2,256,256]{4,3,2,1,0:T(8,128)} %bitcast.44), channel_id=1, replica_groups={{0,1,2,3},{4,5,6,7},{8,9,10,11},{12,13,14,15},{16,17,18,19},{20,21,22,2..., dimensions={0} | all-to-all | bytes 4194304 | tf_op jit(solution)/shard_map/all_to_all | solution.py:563
  393.6 29.1 %all_to_all.41.refs_6_ = f32[4,1,2,256,256]{4,3,2,1,0:T(8,128)} all-to-all(f32[4,1,2,256,256]{4,3,2,1,0:T(8,128)S(1)} %bitcast.43), channel_id=1, replica_groups={{0,1,2,3},{4,5,6,7},{8,9,10,11},{12,13,14,15},{16,17,18,19},{20,21,22,2..., dimensions={0} | all-to-all | bytes 4194304 | tf_op jit(solution)/shard_map/all_to_all | solution.py:563
  422.7 51.8 %all_to_all.42.refs_4_ = f32[4,2,2,256,256]{4,3,2,1,0:T(8,128)} all-to-all(f32[4,2,2,256,256]{4,3,2,1,0:T(8,128)S(1)} %bitcast.38), channel_id=1, replica_groups={{0,1,2,3},{4,5,6,7},{8,9,10,11},{12,13,14,15},{16,17,18,19},{20,21,22,2..., dimensions={0} | all-to-all | bytes 8388608 | tf_op jit(solution)/shard_map/all_to_all | solution.py:563
  474.6 51.8 %all_to_all.43.refs_5_ = f32[4,2,2,256,256]{4,3,2,1,0:T(8,128)} all-to-all(f32[4,2,2,256,256]{4,3,2,1,0:T(8,128)S(1)} %bitcast.40), channel_id=1, replica_groups={{0,1,2,3},{4,5,6,7},{8,9,10,11},{12,13,14,15},{16,17,18,19},{20,21,22,2..., dimensions={0} | all-to-all | bytes 8388608 | tf_op jit(solution)/shard_map/all_to_all | solution.py:563
  526.4 52.0 %all_to_all.44.refs_4_ = f32[4,2,2,256,256]{4,3,2,1,0:T(8,128)} all-to-all(f32[4,2,2,256,256]{4,3,2,1,0:T(8,128)S(1)} %bitcast.37), channel_id=1, replica_groups={{0,1,2,3},{4,5,6,7},{8,9,10,11},{12,13,14,15},{16,17,18,19},{20,21,22,2..., dimensions={0} | all-to-all | bytes 8388608 | tf_op jit(solution)/shard_map/all_to_all | solution.py:563
  578.4 51.9 %all_to_all.45.refs_5_ = f32[4,2,2,256,256]{4,3,2,1,0:T(8,128)} all-to-all(f32[4,2,2,256,256]{4,3,2,1,0:T(8,128)S(1)} %bitcast.39), channel_id=1, replica_groups={{0,1,2,3},{4,5,6,7},{8,9,10,11},{12,13,14,15},{16,17,18,19},{20,21,22,2..., dimensions={0} | all-to-all | bytes 8388608 | tf_op jit(solution)/shard_map/all_to_all | solution.py:563
  630.3 96.8 %all_to_all.46.refs_3_ = f32[4,4,2,256,256]{4,3,2,1,0:T(8,128)} all-to-all(f32[4,4,2,256,256]{4,3,2,1,0:T(8,128)S(1)} %bitcast.35), channel_id=1, replica_groups={{0,1,2,3},{4,5,6,7},{8,9,10,11},{12,13,14,15},{16,17,18,19},{20,21,22,2..., dimensions={0} | all-to-all | bytes 16777216 | tf_op jit(solution)/shard_map/all_to_all | solution.py:563
  727.2 5.0 all-to-all-start.3
  733.5 25.8 %shard_map.113 = f32[8,1,32,4096]{3,2,1,0:T(8,128)} custom-call(f32[2]{0:T(128)} %pad_maximum_fusion.12.refs_0_, bf16[64,256,192]{2,1,0:T(8,128)(2,1)} %pad_maximum_fusion.1.refs_3_.refs_1_, bf16[64,192]{1,0:T(8,128)(2,1)} %pad_maximum_fusion.11.refs_2_, f32[4,4,2,256,256]{4,3,2,1,0:T(8,128)} %all_to_all.46.refs_3_, ...), custom_call_target="tpu_custom_call" | custom-call | flops 20480000000 | bytes 12800000 | tf_op jit(solution)/shard_map/pallas_call | solution.py:459
  759.3 2.4 collective-permute-start
  761.7 25.9 %shard_map.114 = f32[8,1,32,4096]{3,2,1,0:T(8,128)} custom-call(f32[2]{0:T(128)} %pad_maximum_fusion.12.refs_0_, bf16[64,256,192]{2,1,0:T(8,128)(2,1)} %pad_maximum_fusion.1.refs_3_.refs_1_, bf16[64,192]{1,0:T(8,128)(2,1)} %pad_maximum_fusion.11.refs_2_, f32[4,4,2,256,256]{4,3,2,1,0:T(8,128)} %all_to_all.46.refs_3_, ...), custom_call_target="tpu_custom_call" | custom-call | flops 20480000000 | bytes 12800000 | tf_op jit(solution)/shard_map/pallas_call | solution.py:459
  790.8 8.1 all-to-all-done.3.refs_6_
  798.9 45.7 %shard_map.112.refs_0_ = f32[8,2,32,4096]{3,2,1,0:T(8,128)} custom-call(f32[2]{0:T(128)} %pad_maximum_fusion.12.refs_0_, bf16[64,256,192]{2,1,0:T(8,128)(2,1)} %pad_maximum_fusion.1.refs_3_.refs_1_, bf16[64,192]{1,0:T(8,128)(2,1)} %pad_maximum_fusion.11.refs_2_, f32[4,4,2,256,256]{4,3,2,1,0:T(8,128)} %all_to_all.46.refs_3_, ...), custom_call_target="tpu_custom_call" | custom-call | flops 40960000000 | bytes 25600000 | tf_op jit(solution)/shard_map/pallas_call | solution.py:459
  844.6 189.2 %collective-permute-done.refs_1_ = f32[8,1,32,4096]{3,2,1,0:T(8,128)} collective-permute-done((f32[8,1,32,4096]{3,2,1,0:T(8,128)}, f32[8,1,32,4096]{3,2,1,0:T(8,128)}, u32[]{:S(2)}, u32[]{:S(2)}) %collective-permute-start) | collective-permute-done | bytes 4194336 | tf_op jit(solution)/shard_map/ppermute | solution.py:601
  1033.9 89.3 %collective-permute-done.1.refs_2_ = f32[8,1,32,4096]{3,2,1,0:T(8,128)} collective-permute-done((f32[8,1,32,4096]{3,2,1,0:T(8,128)}, f32[8,1,32,4096]{3,2,1,0:T(8,128)}, u32[]{:S(2)}, u32[]{:S(2)}) %collective-permute-start.1) | collective-permute-done | bytes 4194336 | tf_op jit(solution)/shard_map/ppermute | solution.py:601
  1123.2 10.9 shard_map.115
  1138.7 15.8 %all-reduce = f32[16]{0:T(128)S(1)} all-reduce(f32[16]{0:T(128)S(1)} %maximum_dynamic-update-slice_fusion), channel_id=2, replica_groups=mesh['chan'=4,'slab'=8] {'slab'}, use_global_device_ids=true, to_apply=%add | all-reduce | flops 16 | bytes 128
  1156.8 9.9 all-reduce.1
  (76 shorter events, 27.5 us)
Async XLA Ops:
  1.2 42.5 %copy-start.5 = (f32[64,64]{1,0:T(8,128)}, f32[64,64]{1,0:T(8,128)S(1)}, u32[]{:S(2)}) copy-start(f32[64,64]{1,0:T(8,128)S(1)} %get-tuple-element.80) | copy-start | bytes 49156
  1.2 42.5 %copy-start.7 = (f32[64,64]{1,0:T(8,128)}, f32[64,64]{1,0:T(8,128)S(1)}, u32[]{:S(2)}) copy-start(f32[64,64]{1,0:T(8,128)S(1)} %get-tuple-element.79) | copy-start | bytes 49156
  363.1 30.5 %copy-start.4 = (f32[2048,256]{1,0:T(8,128)S(1)}, f32[2048,256]{1,0:T(8,128)}, u32[]{:S(2)}) copy-start(f32[2048,256]{1,0:T(8,128)} %get-tuple-element.35) | copy-start | bytes 6291460
  363.1 59.6 %copy-start.1 = (f32[4096,256]{1,0:T(8,128)S(1)}, f32[4096,256]{1,0:T(8,128)}, u32[]{:S(2)}) copy-start(f32[4096,256]{1,0:T(8,128)} %get-tuple-element.27) | copy-start | bytes 12582916
  422.7 51.8 %copy-start.3 = (f32[4096,256]{1,0:T(8,128)S(1)}, f32[4096,256]{1,0:T(8,128)}, u32[]{:S(2)}) copy-start(f32[4096,256]{1,0:T(8,128)} %get-tuple-element.31) | copy-start | bytes 12582916
  474.6 51.8 %copy-start = (f32[4096,256]{1,0:T(8,128)S(1)}, f32[4096,256]{1,0:T(8,128)}, u32[]{:S(2)}) copy-start(f32[4096,256]{1,0:T(8,128)} %get-tuple-element.26) | copy-start | bytes 12582916
  526.4 52.0 %copy-start.2 = (f32[4096,256]{1,0:T(8,128)S(1)}, f32[4096,256]{1,0:T(8,128)}, u32[]{:S(2)}) copy-start(f32[4096,256]{1,0:T(8,128)} %get-tuple-element.30) | copy-start | bytes 12582916
  526.4 103.9 %slice-start = ((s8[8388608]{0:T(1024)(128)(4,1)}), s8[4194304]{0:T(1024)(128)(4,1)S(1)}, s32[]{:S(2)}) async-start(s8[8388608]{0:T(1024)(128)(4,1)} %bitcast.33), calls=%async_computation.8 | async-start | bytes 8388608
  578.4 51.9 %slice-start.1 = ((s8[8388608]{0:T(1024)(128)(4,1)}), s8[4194304]{0:T(1024)(128)(4,1)S(1)}, s32[]{:S(2)}) async-start(s8[8388608]{0:T(1024)(128)(4,1)} %bitcast.33), calls=%async_computation.9 | async-start | bytes 8388608
  727.2 5.0 copy-start.8
  727.2 5.0 copy-start.6
  727.2 71.7 %all-to-all-start.3 = ((f32[4,2,2,256,256]{4,3,2,1,0:T(8,128)}), f32[4,2,2,256,256]{4,3,2,1,0:T(8,128)}, u32[]{:S(2)}, u32[]{:S(2)}) async-start(f32[4,2,2,256,256]{4,3,2,1,0:T(8,128)} %bitcast.36), calls=%async_computation.3 | async-start | bytes 8388608 | tf_op jit(solution)/shard_map/all_to_all | solution.py:563
  759.3 28.9 %copy-start.10 = (u32[32]{0:T(128)S(1)}, u32[32]{0:T(128)}, u32[]{:S(2)}) copy-start(u32[32]{0:T(128)} %constant.187) | copy-start | bytes 388
  759.3 29.5 %copy-start.9 = (u32[32]{0:T(128)S(1)}, u32[32]{0:T(128)}, u32[]{:S(2)}) copy-start(u32[32]{0:T(128)} %constant.182) | copy-start | bytes 388
  759.3 274.5 %collective-permute-start = (f32[8,1,32,4096]{3,2,1,0:T(8,128)}, f32[8,1,32,4096]{3,2,1,0:T(8,128)}, u32[]{:S(2)}, u32[]{:S(2)}) collective-permute-start(f32[8,1,32,4096]{3,2,1,0:T(8,128)} %shard_map.113), channel_id=1, source_target_pairs={{0,4},{1,5},{2,6},{3,7},{4,0},{5,1},{6,2},{7,3},{8,12},{9,13},{10,... | collective-permute-start | bytes 12582920 | tf_op jit(solution)/shard_map/ppermute | solution.py:601
  787.6 335.6 %collective-permute-start.1 = (f32[8,1,32,4096]{3,2,1,0:T(8,128)}, f32[8,1,32,4096]{3,2,1,0:T(8,128)}, u32[]{:S(2)}, u32[]{:S(2)}) collective-permute-start(f32[8,1,32,4096]{3,2,1,0:T(8,128)} %shard_map.114), channel_id=1, source_target_pairs={{0,4},{1,5},{2,6},{3,7},{4,0},{5,1},{6,2},{7,3},{8,12},{9,13},{10,... | collective-permute-start | bytes 12582920 | tf_op jit(solution)/shard_map/ppermute | solution.py:601
